TPU v7x, 32 devices: a whole 2x2x4 slice. The times are simulated.
32 devices in a mesh: groups: 2 (over x), tile: 16 (over z, y, core).
Axes of the slice: x: 2, y: 2, z: 4, core: 2. Of those that a mesh axis runs over, the one named last changes fastest.
Arguments:
- echoes: float32 [2, 32, 16384], P(None, ('groups', 'tile')), parts along dimension 1, may hold values from -6 to 6
- bin_start: int32 [32, 16], P(('groups', 'tile')), parts along dimension 0, may hold values from 0 to 16128
- bin_fraction: float32 [16, 32], P(None, ('groups', 'tile')), parts along dimension 1, may hold values from 0 to 1
- row_phase: float32 [16, 32, 128], P(None, ('groups', 'tile')), parts along dimension 1, may hold values from -3.140625 to 3.140625
- column_phase: float32 [16, 32, 128], P(None, ('groups', 'tile')), parts along dimension 1, may hold values from -3.140625 to 3.140625
- row_bin: int32 [16, 32, 128], P(None, ('groups', 'tile')), parts along dimension 1, may hold values from 0 to 127
- column_bin: int32 [16, 32, 128], P(None, ('groups', 'tile')), parts along dimension 1, may hold values from 0 to 127
Outputs:
- focused: float32 [2, 32, 128, 128], P(None, ('groups', 'tile')), parts along dimension 1
- correction: float32 [2, 32], P(None, ('groups', 'tile')), parts along dimension 1
There are 2 independent parts, one for each index of `groups`. A program takes and returns all parts, laid end to end along the dimension named above; each array names one. Nothing has to cross between parts.
Inputs may be any that keep to these rules, and one draw needn't show every extreme that they name: The window of 256 range bins that begins at bin_start lies within the 16384 bins.
All inputs are finite; a program needn't handle non-finite values.
Results may differ from a plain program's by a relative error of at most 0.012.
Values may be sent and summed in bfloat16 or wider, within the bound.
A program may use at most 320 MiB of HBM per device.

v0:
```python
import functools
import math

import jax
import jax.numpy as jnp
import numpy as np
from jax import lax
from jax.experimental import pallas as pl
from jax.experimental.pallas import tpu as pltpu
from jax.sharding import PartitionSpec as P

LANES = 128
OCTET = 8
MESH = pl.DeviceIdType.MESH
F32 = jnp.float32
BF16 = jnp.bfloat16


def tables(samples):
    inner = LANES
    outer = samples // inner

    def wave(rows, columns, period):
        product = np.arange(rows)[:, None] * np.arange(columns)[None, :] % period
        phases = product * (2.0 * np.pi / period)
        return np.cos(phases), np.sin(phases)

    def split(table):
        table = table.astype(np.float32)
        high = table.astype(jnp.bfloat16)
        low = (table - high.astype(np.float32)).astype(jnp.bfloat16)
        return np.stack([high, low])

    first = split(np.concatenate(wave(outer, outer, outer), 1))
    last = split(np.concatenate(wave(inner, inner, inner), 1))
    turn = np.stack(wave(outer, inner, samples)) / math.sqrt(samples)
    return first, turn.astype(np.float32), last


def fold_table(pulses):
    block = np.arange(pulses * 2 * OCTET) // OCTET
    pulse, part = block // 2, block % 2
    lane = np.arange(LANES)
    same = [(lane[None, :] == pulse[:, None] + shift * pulses) for shift in (0, 1)]
    real_in = part[:, None] == 0
    real_rows = (same[0] & real_in) * 1.0 + (same[1] & ~real_in) * 1.0
    imag_rows = (same[0] & ~real_in) * 1.0 - (same[1] & real_in) * 1.0
    return np.stack([real_rows, imag_rows]).astype(np.float32)


def dot(a, b, dims=((1,), (0,)), precision=None):
    return lax.dot_general(a, b, (dims, ((), ())), precision=precision, preferred_element_type=F32)


def split3(table_ref, data, dims):
    high = data.astype(BF16)
    low = (data - high.astype(F32)).astype(BF16)
    return dot(table_ref[0], high, dims) + (dot(table_ref[1], high, dims) + dot(table_ref[0], low, dims))


def normalize(real_part, imag_part, axis, count):
    magnitude = real_part * real_part + imag_part * imag_part
    mean = jnp.sum(magnitude, axis=axis, keepdims=True) / count
    denominator = jnp.sqrt(magnitude + mean + 1e-06)
    return real_part / denominator, imag_part / denominator


def kernel(
    n, starts_in, echo_in, first_in, turn_in, last_in, row_phase_in, column_phase_in, row_bin_in, column_bin_in,
    fraction_in, fold_in,
    focused, correction,
    starts, echo, first, turn, last, row_phase, column_phase, row_bin, column_bin, fraction, fold, in_sem,
    spec, outgoing, gathered, steer, parts, gram_in, message, messages, weights,
    send_sem, recv_sem, send_sem2, recv_sem2,
):
    me = lax.axis_index("tile")
    rows = row_phase.shape[2]
    scale = 1.0 / math.sqrt(n)

    barrier = pltpu.get_barrier_semaphore()
    for k in range(1, n):
        pl.semaphore_signal(barrier, inc=1, device_id={"tile": lax.rem(me + k, n)}, device_id_type=MESH)

    sources = (
        starts_in, echo_in, first_in, turn_in, last_in, row_phase_in, column_phase_in, row_bin_in, column_bin_in,
        fraction_in, fold_in,
    )
    targets = (starts, echo, first, turn, last, row_phase, column_phase, row_bin, column_bin, fraction, fold)
    loads = [
        pltpu.make_async_copy(source, target, in_sem.at[i])
        for i, (source, target) in enumerate(zip(sources, targets))
    ]
    for load in loads[1:] + loads[:1]:
        load.start()

    upper = (2 * me) // n

    def other(k):
        place = upper * k + (1 - upper) * (n - 2 - k)
        return place + (place >= me).astype(jnp.int32)


    loads[1].wait()
    loads[2].wait()
    real, imag = echo[0], echo[1]
    data = jnp.concatenate(
        [jnp.concatenate([real, imag], 1), jnp.concatenate([imag, -real], 1)], 0
    )
    section = split3(first, data, ((1,), (0,)))
    half = section.shape[1] // 2
    loads[3].wait()
    loads[4].wait()
    real, imag = section[:, :half], section[:, half:]
    turned_real = real * turn[0] + imag * turn[1]
    turned_imag = imag * turn[0] - real * turn[1]
    data = jnp.concatenate(
        [jnp.concatenate([turned_real, turned_imag], 1), jnp.concatenate([turned_imag, -turned_real], 1)], 0
    )
    spectrum = split3(last, data, ((1,), (1,)))
    bins = spectrum.shape[0]
    spectrum = spectrum.astype(BF16).astype(F32)
    for h in range(2):
        spec[h, 0:bins, :] = spectrum[:, h * LANES : (h + 1) * LANES]
        spec[h, bins:, :] = jnp.zeros((spec.shape[1] - bins, LANES), F32)

    lane = lax.broadcasted_iota(jnp.int32, (OCTET, LANES), 1)
    loads[0].wait()
    for t in range(n):
        start = starts[0, t]
        top = start // LANES
        left = LANES - start % LANES
        pieces = []
        for h in range(2):
            moved = pltpu.roll(spec[h, pl.ds(top, OCTET), :], left % LANES, 1)
            below = pltpu.roll(moved, OCTET - 1, 0)
            pieces.append(jnp.where(lane < left, moved, below)[0:2])
        outgoing[t] = jnp.concatenate(pieces, 0).astype(BF16)

    pl.semaphore_wait(barrier, n - 1)

    def window_copy(device, slot):
        return pltpu.make_async_remote_copy(
            src_ref=outgoing.at[device],
            dst_ref=gathered.at[slot],
            send_sem=send_sem.at[device],
            recv_sem=recv_sem.at[slot],
            device_id={"tile": device},
            device_id_type=MESH,
        )

    for k in range(n - 1):
        window_copy(other(k), me).start()
    gathered[me] = outgoing[me]

    def rounded(values):
        return values.astype(BF16).astype(F32)

    for load in loads[5:]:
        load.wait()
    angles = row_phase[:, 0, :]
    left_side = jnp.concatenate(
        [
            rounded(jnp.cos(angles)),
            rounded(jnp.sin(angles)),
            row_bin[:, 0, :].astype(F32),
            jnp.ones((n, rows), F32),
        ],
        0,
    )
    left_side = left_side.T.astype(BF16)
    angles = column_phase[:, 0, :]
    cosine, sine = rounded(jnp.cos(angles)), rounded(jnp.sin(angles))
    zero, one = jnp.zeros((n, LANES), F32), jnp.ones((n, LANES), F32)
    right_side = jnp.concatenate(
        [
            jnp.concatenate([cosine, sine, zero], 1),
            jnp.concatenate([-sine, cosine, zero], 1),
            jnp.concatenate([zero, zero, one], 1),
            jnp.concatenate([zero, zero, column_bin[:, 0, :].astype(F32)], 1),
        ],
        0,
    )
    owner = lax.rem(lax.broadcasted_iota(jnp.int32, right_side.shape, 0), n)
    for p in range(n):
        steer[p] = dot(left_side, jnp.where(owner == p, right_side, 0.0).astype(BF16))

    lane4 = lax.broadcasted_iota(jnp.int32, (4, LANES), 1)

    def contribute(p):
        window = gathered[p].astype(F32)
        moved = pltpu.roll(window, LANES - 1, 1)
        below = jnp.concatenate([moved[1:4], moved[0:1]], 0)
        shifted = jnp.where(lane4 == LANES - 1, below, moved)
        share = fraction[0, p]
        profile = ((1.0 - share) * window + share * shifted).astype(BF16).astype(F32)
        index = steer[p, :, 2 * LANES :].astype(jnp.int32)
        low = index < LANES
        index = index & (LANES - 1)

        def pick(row):
            source = jnp.broadcast_to(profile[row : row + 1, :], (rows, LANES))
            return jnp.take_along_axis(source, index, axis=1, mode="promise_in_bounds")

        real = jnp.where(low, pick(0), pick(1))
        imag = jnp.where(low, pick(2), pick(3))
        turn_real, turn_imag = steer[p, :, :LANES], steer[p, :, LANES : 2 * LANES]
        part_real = turn_real * real - turn_imag * imag
        part_imag = turn_real * imag + turn_imag * real
        parts[p, 0] = part_real
        parts[p, 1] = part_imag
        own_rows = pl.ds(pl.multiple_of(p * 2 * OCTET, 2 * OCTET), 2 * OCTET)
        for t in range(rows // OCTET):
            pair = jnp.concatenate(
                [part_real[t * OCTET : (t + 1) * OCTET], part_imag[t * OCTET : (t + 1) * OCTET]], 0
            )
            gram_in[own_rows, t * LANES : (t + 1) * LANES] = pair.astype(BF16)

    contribute(me)
    near_first = [other(k) for k in reversed(range(n - 1))]
    cuts = [0, n // 2 - 1, 3 * n // 4 - 1, n - 1]
    for begin, end in zip(cuts[:-1], cuts[1:]):
        for device in near_first[begin:end]:
            window_copy(device, device).wait()
        for device in near_first[begin:end]:
            contribute(device)

    values = gram_in[...]
    product = dot(values, values, ((1,), (1,)))
    row_id = lax.broadcasted_iota(jnp.int32, product.shape, 0)
    column_id = lax.broadcasted_iota(jnp.int32, product.shape, 1)
    product = jnp.where(lax.rem(row_id, OCTET) == lax.rem(column_id, OCTET), product, 0.0)
    product = product.reshape(n, 2, OCTET, product.shape[1])
    gram = dot(jnp.sum(product[:, 0], axis=1), fold[0], precision=lax.Precision.HIGHEST)
    gram = gram + dot(jnp.sum(product[:, 1], axis=1), fold[1], precision=lax.Precision.HIGHEST)
    groups = LANES // (2 * n)
    depth = n // groups
    packed = gram[0:depth]
    for g in range(1, groups):
        packed = packed + pltpu.roll(gram[g * depth : (g + 1) * depth], g * 2 * n, 1)
    message[...] = packed
    messages[me] = packed

    def gram_copy(device, slot):
        return pltpu.make_async_remote_copy(
            src_ref=message,
            dst_ref=messages.at[slot],
            send_sem=send_sem2.at[device],
            recv_sem=recv_sem2.at[slot],
            device_id={"tile": device},
            device_id_type=MESH,
        )

    for k in range(n - 1):
        gram_copy(other(k), me).start()
    for device in near_first:
        gram_copy(device, device).wait()

    total = jnp.sum(messages[...], axis=0)
    gram = jnp.concatenate(
        [total] + [pltpu.roll(total, LANES - g * 2 * n, 1) for g in range(1, groups)], 0
    )
    row_id = lax.broadcasted_iota(jnp.int32, gram.shape, 0)
    column_id = lax.broadcasted_iota(jnp.int32, gram.shape, 1)
    off_diagonal = (column_id < n) & (column_id != row_id)
    gram_real = jnp.where(off_diagonal, gram * scale, 0.0)
    gram_imag = jnp.where(off_diagonal, pltpu.roll(gram, LANES - n, 1) * scale, 0.0)

    def along(values, axis):
        return jnp.sum(values, axis=axis, keepdims=True)

    one_real, one_imag = normalize(along(gram_real, 1), along(gram_imag, 1), 0, n)
    row_real, row_imag = normalize(along(gram_real, 0), -along(gram_imag, 0), 1, n)
    rest_real = along(gram_real * row_real - gram_imag * row_imag, 1)
    rest_imag = along(gram_real * row_imag + gram_imag * row_real, 1)
    again_real = one_real * rest_real + one_imag * rest_imag
    again_imag = one_real * rest_imag - one_imag * rest_real
    two_real, two_imag = normalize(again_real, again_imag, 0, n)
    total_real = one_real * two_real - one_imag * two_imag
    total_imag = one_real * two_imag + one_imag * two_real
    mine = lax.broadcasted_iota(jnp.int32, total_real.shape, 0) == me
    own_real = along(jnp.where(mine, total_real, 0.0), 0)
    own_imag = along(jnp.where(mine, total_imag, 0.0), 0)
    correction[...] = jnp.concatenate([own_real, own_imag], 1)
    weights[0] = jnp.broadcast_to(total_real * scale, (n, LANES))
    weights[1] = jnp.broadcast_to(total_imag * scale, (n, LANES))

    step = 4 * OCTET
    for t in range(rows // step):
        span = slice(t * step, (t + 1) * step)
        sum_real = jnp.zeros((step, LANES), F32)
        sum_imag = jnp.zeros((step, LANES), F32)
        for p in range(n):
            weight_real = weights[0, p : p + 1, :]
            weight_imag = weights[1, p : p + 1, :]
            part_real, part_imag = parts[p, 0, span, :], parts[p, 1, span, :]
            sum_real = sum_real + (weight_real * part_real - weight_imag * part_imag)
            sum_imag = sum_imag + (weight_real * part_imag + weight_imag * part_real)
        focused[0, 0, span, :] = sum_real
        focused[1, 0, span, :] = sum_imag


def solution(mesh):
    n = mesh.shape["tile"]

    def per_device(echoes, bin_start, bin_fraction, row_phase, column_phase, row_bin, column_bin):
        samples = echoes.shape[2]
        rows, columns = row_phase.shape[2], column_phase.shape[2]
        first, turn, last = tables(samples)
        bins = samples // LANES
        echo = echoes.reshape(2, bins, LANES)
        fold = fold_table(n)
        vmem = pl.BlockSpec(memory_space=pltpu.VMEM)
        operands = (
            bin_start, echo, jnp.asarray(first), jnp.asarray(turn), jnp.asarray(last),
            row_phase, column_phase, row_bin, column_bin, bin_fraction.T, jnp.asarray(fold),
        )
        depth = n * 2 * n // LANES
        focused, correction = pl.pallas_call(
            functools.partial(kernel, n),
            out_shape=(
                pltpu.VMEM((2, 1, rows, columns), F32),
                pltpu.VMEM((1, 2), F32),
            ),
            in_specs=[pl.BlockSpec(memory_space=pltpu.HBM)] * len(operands),
            out_specs=(vmem, vmem),
            scratch_shapes=[pltpu.SMEM(bin_start.shape, jnp.int32)]
            + [pltpu.VMEM(operand.shape, operand.dtype) for operand in operands[1:9]]
            + [pltpu.SMEM((1, n), F32), pltpu.VMEM(fold.shape, F32), pltpu.SemaphoreType.DMA((len(operands),))]
            + [
                pltpu.VMEM((2, bins + OCTET, LANES), F32),
                pltpu.VMEM((n, 4, LANES), BF16),
                pltpu.VMEM((n, 4, LANES), BF16),
                pltpu.VMEM((n, rows, 3 * LANES), F32),
                pltpu.VMEM((n, 2, rows, columns), F32),
                pltpu.VMEM((n * 2 * OCTET, rows // OCTET * columns), BF16),
                pltpu.VMEM((depth, LANES), F32),
                pltpu.VMEM((n, depth, LANES), F32),
                pltpu.VMEM((2, n, LANES), F32),
                pltpu.SemaphoreType.DMA((n,)),
                pltpu.SemaphoreType.DMA((n,)),
                pltpu.SemaphoreType.DMA((n,)),
                pltpu.SemaphoreType.DMA((n,)),
            ],
            compiler_params=pltpu.CompilerParams(collective_id=0, has_side_effects=True),
        )(*operands)
        return focused, correction.T

    split = ("groups", "tile")
    in_specs = (
        P(None, split, None),
        P(split, None),
        P(None, split),
        P(None, split, None),
        P(None, split, None),
        P(None, split, None),
        P(None, split, None),
    )
    out_specs = (P(None, split, None, None), P(None, split))
    return jax.shard_map(per_device, mesh=mesh, in_specs=in_specs, out_specs=out_specs, check_vma=False)
```

profile of v0, /device:TPU:0, one launch (start us, length us, event | category | flops | bytes accessed | tf_op | source)
XLA Modules:
  0.0 20.1 jit_solution(8065567387567028281)
XLA Ops:
  0.6 18.3 %shard_map.122 = (f32[2,1,128,128]{3,2,1,0:T(8,128)S(1)}, f32[1,2]{1,0:T(1,128)S(1)}) custom-call(s32[1,16]{1,0:T(1,128)} %starts_in.1, f32[2,128,128]{2,1,0:T(8,128)} %bitcast.4, bf16[2,128,256]{2,1,0:T(8,128)(2,1)} %constant.6.clone.first_in.last_in, f32[2,128,128]{2,1,0:T(8,128)} %constant.7.clone.turn_in, ...), custom_call_target="tpu_custom_call" | custom-call | tf_op jit(solution)/shard_map/pallas_call | solution.py:318
  18.9 0.7 %copy.15 = f32[2,1,128,128]{3,2,1,0:T(8,128)} copy(f32[2,1,128,128]{3,2,1,0:T(8,128)S(1)} %get-tuple-element.6) | data formatting | bytes 262144
  19.6 0.5 %copy.16 = f32[2,1]{0,1:T(1,128)} copy(f32[2,1]{0,1:T(1,128)S(1)} %bitcast.3) | data formatting | bytes 16
where the time goes:
time: 20.3 us; the launch traced here: 20.1 us
  Pallas kernels  18.3 us (90%)
  local copies, waits for them, and re-layouts  1.17 us (6%)
  between operations  0.64 us (3%)
    pallas_call x1, Pallas kernels, per_device(): pl.pallas_call(functools.partial(kernel, n), out_shape=(pltpu.VMEM((2, 1,...  18.3 us
    unnamed x2, local copies, waits for them, and re-layouts  1.17 us

commit v1 on v0

v1 whole, which is shorter than its diff:
```python
import functools
import math

import jax
import jax.numpy as jnp
import numpy as np
from jax import lax
from jax.experimental import pallas as pl
from jax.experimental.pallas import tpu as pltpu
from jax.sharding import PartitionSpec as P

LANES = 128
OCTET = 8
MESH = pl.DeviceIdType.MESH
F32 = jnp.float32
BF16 = jnp.bfloat16


def tables(samples):
    inner = LANES
    outer = samples // inner

    def wave(rows, columns, period):
        product = np.arange(rows)[:, None] * np.arange(columns)[None, :] % period
        phases = product * (2.0 * np.pi / period)
        return np.cos(phases), np.sin(phases)

    def split(table):
        table = table.astype(np.float32)
        high = table.astype(jnp.bfloat16)
        low = (table - high.astype(np.float32)).astype(jnp.bfloat16)
        return np.stack([high, low])

    first = split(np.concatenate(wave(outer, outer, outer), 1))
    last = split(np.concatenate(wave(inner, inner, inner), 1))
    turn = np.stack(wave(outer, inner, samples)) / math.sqrt(samples)
    return first, turn.astype(np.float32), last


def dot(a, b, dims=((1,), (0,)), precision=None):
    return lax.dot_general(a, b, (dims, ((), ())), precision=precision, preferred_element_type=F32)


def split3(table_ref, data, dims):
    high = data.astype(BF16)
    low = (data - high.astype(F32)).astype(BF16)
    return dot(table_ref[0], high, dims) + (dot(table_ref[1], high, dims) + dot(table_ref[0], low, dims))


def normalize(real_part, imag_part, axis, count):
    magnitude = real_part * real_part + imag_part * imag_part
    mean = jnp.sum(magnitude, axis=axis, keepdims=True) / count
    denominator = jnp.sqrt(magnitude + mean + 1e-06)
    return real_part / denominator, imag_part / denominator


def pick(source, index):
    numbers = lax.GatherDimensionNumbers(
        offset_dims=(), collapsed_slice_dims=(1,), start_index_map=(1,),
        operand_batching_dims=(0,), start_indices_batching_dims=(0,),
    )
    return lax.gather(
        source, index[..., None], numbers, (1, 1), mode=lax.GatherScatterMode.PROMISE_IN_BOUNDS
    )


def kernel(
    n, starts_in, echo_in, first_in, turn_in, last_in, row_phase_in, column_phase_in, row_bin_in, column_bin_in,
    fraction_in,
    focused, correction,
    starts, echo, first, turn, last, row_phase, column_phase, row_bin, column_bin, fraction, in_sem,
    spec, outgoing, gathered, waves, bins_of, share, index_low, index_all, steer, windows, parts,
    gram_rows, message, messages,
    send_sem, recv_sem, send_sem2, recv_sem2,
):
    me = lax.axis_index("tile")
    rows = row_phase.shape[2]
    scale = 1.0 / math.sqrt(n)
    groups = n // OCTET
    mine = me // OCTET
    pair = 2 * n

    def group_of(slot):
        return lax.rem(mine + slot, groups)

    barrier = pltpu.get_barrier_semaphore()
    for k in range(1, n):
        pl.semaphore_signal(barrier, inc=1, device_id={"tile": lax.rem(me + k, n)}, device_id_type=MESH)

    sources = (
        starts_in, echo_in, first_in, turn_in, last_in, row_phase_in, column_phase_in, row_bin_in, column_bin_in,
        fraction_in,
    )
    targets = (starts, echo, first, turn, last, row_phase, column_phase, row_bin, column_bin, fraction)
    loads = [
        pltpu.make_async_copy(source, target, in_sem.at[i])
        for i, (source, target) in enumerate(zip(sources, targets))
    ]
    for load in loads[1:] + loads[:1]:
        load.start()

    upper = (2 * me) // n

    def other(k):
        place = upper * k + (1 - upper) * (n - 2 - k)
        return place + (place >= me).astype(jnp.int32)


    loads[1].wait()
    loads[2].wait()
    real, imag = echo[0], echo[1]
    data = jnp.concatenate(
        [jnp.concatenate([real, imag], 1), jnp.concatenate([imag, -real], 1)], 0
    )
    section = split3(first, data, ((1,), (0,)))
    half = section.shape[1] // 2
    loads[3].wait()
    loads[4].wait()
    real, imag = section[:, :half], section[:, half:]
    turned_real = real * turn[0] + imag * turn[1]
    turned_imag = imag * turn[0] - real * turn[1]
    data = jnp.concatenate(
        [jnp.concatenate([turned_real, turned_imag], 1), jnp.concatenate([turned_imag, -turned_real], 1)], 0
    )
    spectrum = split3(last, data, ((1,), (1,)))
    bins = spectrum.shape[0]
    spectrum = spectrum.astype(BF16).astype(F32)
    for h in range(2):
        spec[h, 0:bins, :] = spectrum[:, h * LANES : (h + 1) * LANES]
        spec[h, bins:, :] = jnp.zeros((spec.shape[1] - bins, LANES), F32)

    lane = lax.broadcasted_iota(jnp.int32, (OCTET, LANES), 1)
    loads[0].wait()
    for t in range(n):
        start = starts[0, t]
        top = start // LANES
        left = LANES - start % LANES
        pieces = []
        for h in range(2):
            moved = pltpu.roll(spec[h, pl.ds(top, OCTET), :], left % LANES, 1)
            below = pltpu.roll(moved, OCTET - 1, 0)
            pieces.append(jnp.where(lane < left, moved, below)[0:2])
        outgoing[t] = jnp.concatenate(pieces, 0).astype(BF16)

    pl.semaphore_wait(barrier, n - 1)

    def window_copy(device, slot):
        return pltpu.make_async_remote_copy(
            src_ref=outgoing.at[device],
            dst_ref=gathered.at[slot],
            send_sem=send_sem.at[device],
            recv_sem=recv_sem.at[slot],
            device_id={"tile": device},
            device_id_type=MESH,
        )

    for k in range(n - 1):
        window_copy(other(k), me).start()
    gathered[me] = outgoing[me]

    def rounded(values):
        return values.astype(BF16).astype(F32)

    for load in loads[5:]:
        load.wait()

    def by_octets(values):
        return values.reshape(groups, OCTET, LANES)

    angles = row_phase[:, 0, :]
    waves[0] = by_octets(rounded(jnp.cos(angles)))
    waves[1] = by_octets(rounded(jnp.sin(angles)))
    angles = column_phase[:, 0, :]
    waves[2] = by_octets(rounded(jnp.cos(angles)))
    waves[3] = by_octets(rounded(jnp.sin(angles)))
    bins_of[0] = by_octets(row_bin[:, 0, :])
    bins_of[1] = by_octets(column_bin[:, 0, :])
    octet_id = lax.broadcasted_iota(jnp.int32, (OCTET, LANES), 0)
    tiles = rows // OCTET

    def spread(values, u):
        return jnp.broadcast_to(values[:, u : u + 1], (OCTET, LANES))

    for slot in range(groups):
        group = group_of(slot)
        part = jnp.zeros((OCTET, LANES), F32)
        for i in range(OCTET):
            part = jnp.where(octet_id == i, fraction[0, group * OCTET + i], part)
        share[slot] = part
        row_cosine, row_sine = waves[0, group], waves[1, group]
        column_cosine, column_sine = waves[2, group], waves[3, group]
        row_index, column_index = bins_of[0, group], bins_of[1, group]
        for u in range(rows):
            cosine, sine = spread(row_cosine, u), spread(row_sine, u)
            index = spread(row_index, u) + column_index
            index_all[slot, u] = index
            index_low[slot, u] = index & (LANES - 1)
            steer[0, slot, u] = cosine * column_cosine - sine * column_sine
            steer[1, slot, u] = cosine * column_sine + sine * column_cosine

    def contribute(slot):
        group = group_of(slot)
        for i in range(OCTET):
            windows[slot, 4 * i : 4 * (i + 1), :] = gathered[group * OCTET + i].astype(F32)
        window = [windows[slot, pl.ds(q, OCTET, stride=4), :] for q in range(4)]
        moved = [pltpu.roll(values, LANES - 1, 1) for values in window]
        fraction_of = share[slot]
        profile = []
        for q in range(4):
            shifted = moved[q] if q % 2 else jnp.where(lane == LANES - 1, moved[q + 1], moved[q])
            profile.append(rounded((1.0 - fraction_of) * window[q] + fraction_of * shifted))
        for u in range(rows):
            low = index_low[slot, u]
            is_low = index_all[slot, u] < LANES
            real = jnp.where(is_low, pick(profile[0], low), pick(profile[1], low))
            imag = jnp.where(is_low, pick(profile[2], low), pick(profile[3], low))
            turn_real, turn_imag = steer[0, slot, u], steer[1, slot, u]
            both = jnp.concatenate([turn_real * real - turn_imag * imag, turn_real * imag + turn_imag * real], 0)
            top = (u % OCTET) * pair + slot * 2 * OCTET
            left = (u // OCTET) * LANES
            parts[top : top + 2 * OCTET, left : left + LANES] = both.astype(BF16)

    for slot in range(groups):
        for k in range(1 if slot == 0 else 0, OCTET):
            device = group_of(slot) * OCTET + lax.rem(me + k, OCTET)
            window_copy(device, device).wait_recv()
        contribute(slot)

    total = None
    for top in range(0, OCTET * pair, LANES):
        values = parts[top : top + LANES, :]
        product = dot(values, values, ((1,), (1,)))
        total = product if total is None else total + product
    gram = total[0:pair]
    for i in range(1, LANES // pair):
        gram = gram + pltpu.roll(total[i * pair : (i + 1) * pair], LANES - i * pair, 1)
    imag_lane = (lane // OCTET) % 2 == 1
    for slot in range(groups):
        top = slot * 2 * OCTET
        real, imag = gram[top : top + OCTET], gram[top + OCTET : top + 2 * OCTET]
        values = real + jnp.where(
            imag_lane, -pltpu.roll(imag, OCTET, 1), pltpu.roll(imag, LANES - OCTET, 1)
        )
        values = jnp.where(lane < pair, values, 0.0)
        width = pair
        while width < LANES:
            values = values + pltpu.roll(values, width, 1)
            width *= 2
        gram_rows[group_of(slot)] = pltpu.roll(values, 2 * OCTET * mine, 1)
    full = gram_rows[...].reshape(n, LANES)
    depth = n * pair // LANES
    folds = LANES // pair
    block_id = lax.broadcasted_iota(jnp.int32, (depth, LANES), 1) // pair
    packed = full[0:depth]
    for j in range(1, folds):
        packed = jnp.where(block_id == j, full[j * depth : (j + 1) * depth], packed)
    message[...] = packed
    messages[me] = packed

    def gram_copy(device, slot):
        return pltpu.make_async_remote_copy(
            src_ref=message,
            dst_ref=messages.at[slot],
            send_sem=send_sem2.at[device],
            recv_sem=recv_sem2.at[slot],
            device_id={"tile": device},
            device_id_type=MESH,
        )

    for k in range(n - 1):
        gram_copy(other(k), me).start()
    for k in range(n - 1):
        window_copy(other(k), me).wait_send()
    for k in reversed(range(n - 1)):
        gram_copy(other(k), other(k)).wait_recv()

    total = jnp.sum(messages[...], axis=0)
    gram = jnp.concatenate([total] + [pltpu.roll(total, LANES - j * pair, 1) for j in range(1, folds)], 0)
    row_id = lax.broadcasted_iota(jnp.int32, gram.shape, 0)
    lane_id = lax.broadcasted_iota(jnp.int32, gram.shape, 1)
    column_id = lane_id // (2 * OCTET) * OCTET + lane_id % OCTET
    off_diagonal = (lane_id < pair) & (lane_id // OCTET % 2 == 0) & (column_id != row_id)
    gram_real = jnp.where(off_diagonal, gram * scale, 0.0)
    gram_imag = jnp.where(off_diagonal, pltpu.roll(gram, LANES - OCTET, 1) * scale, 0.0)

    def along(values, axis):
        return jnp.sum(values, axis=axis, keepdims=True)

    one_real, one_imag = normalize(along(gram_real, 1), along(gram_imag, 1), 0, n)
    row_real, row_imag = normalize(along(gram_real, 0), -along(gram_imag, 0), 1, n)
    rest_real = along(gram_real * one_real + gram_imag * one_imag, 0)
    rest_imag = along(gram_real * one_imag - gram_imag * one_real, 0)
    again_real = row_real * rest_real + row_imag * rest_imag
    again_imag = row_real * rest_imag - row_imag * rest_real
    two_real, two_imag = normalize(again_real, again_imag, 1, n)
    total_real = row_real * two_real - row_imag * two_imag
    total_imag = row_real * two_imag + row_imag * two_real
    lane_row = lax.broadcasted_iota(jnp.int32, total_real.shape, 1)
    own_lane = (me // OCTET) * 2 * OCTET + me % OCTET
    own = lane_row == own_lane
    correction[...] = jnp.concatenate(
        [along(jnp.where(own, total_real, 0.0), 1), along(jnp.where(own, total_imag, 0.0), 1)], 1
    )
    row_parts = (lane_row // OCTET) % 2 == 1
    weights = []
    for values in (
        jnp.where(row_parts, -pltpu.roll(total_imag, OCTET, 1), total_real),
        jnp.where(row_parts, pltpu.roll(total_real, OCTET, 1), total_imag),
    ):
        values = jnp.where(lane_row < pair, values * scale, 0.0)
        width = pair
        while width < LANES:
            values = values + pltpu.roll(values, width, 1)
            width *= 2
        values = pltpu.roll(values, LANES - 2 * OCTET * mine, 1)
        weights.append(jnp.broadcast_to(values, (OCTET, LANES)))
    weights = jnp.concatenate(weights, 0)
    phase_id = lax.broadcasted_iota(jnp.int32, weights.shape, 0) % OCTET
    weight_lane = lax.broadcasted_iota(jnp.int32, weights.shape, 1)
    spans = [
        jnp.where((weight_lane + left) // pair == phase_id, weights, 0.0) for left in range(0, OCTET * pair, LANES)
    ]
    weights = jnp.concatenate(spans, 1)
    high = weights.astype(BF16)
    low = (weights - high.astype(F32)).astype(BF16)
    weights = jnp.concatenate([high, low], 0)
    step = 2 * LANES
    for left in range(0, tiles * LANES, step):
        image = dot(weights, parts[:, left : left + step])
        image = image[0 : 2 * OCTET] + image[2 * OCTET :]
        for i in range(step // LANES):
            t = left // LANES + i
            span = slice(t * OCTET, (t + 1) * OCTET)
            for h in range(2):
                focused[h, 0, span, :] = image[h * OCTET : (h + 1) * OCTET, i * LANES : (i + 1) * LANES]

    for k in range(n - 1):
        gram_copy(other(k), me).wait_send()


def solution(mesh):
    n = mesh.shape["tile"]

    def per_device(echoes, bin_start, bin_fraction, row_phase, column_phase, row_bin, column_bin):
        samples = echoes.shape[2]
        rows, columns = row_phase.shape[2], column_phase.shape[2]
        first, turn, last = tables(samples)
        bins = samples // LANES
        echo = echoes.reshape(2, bins, LANES)
        vmem = pl.BlockSpec(memory_space=pltpu.VMEM)
        operands = (
            bin_start, echo, jnp.asarray(first), jnp.asarray(turn), jnp.asarray(last),
            row_phase, column_phase, row_bin, column_bin, bin_fraction.T,
        )
        depth = n * 2 * n // LANES
        focused, correction = pl.pallas_call(
            functools.partial(kernel, n),
            out_shape=(
                pltpu.VMEM((2, 1, rows, columns), F32),
                pltpu.VMEM((1, 2), F32),
            ),
            in_specs=[pl.BlockSpec(memory_space=pltpu.HBM)] * len(operands),
            out_specs=(vmem, vmem),
            scratch_shapes=[pltpu.SMEM(bin_start.shape, jnp.int32)]
            + [pltpu.VMEM(operand.shape, operand.dtype) for operand in operands[1:9]]
            + [pltpu.SMEM((1, n), F32), pltpu.SemaphoreType.DMA((len(operands),))]
            + [
                pltpu.VMEM((2, bins + OCTET, LANES), F32),
                pltpu.VMEM((n, 4, LANES), BF16),
                pltpu.VMEM((n, 4, LANES), BF16),
                pltpu.VMEM((4, n // OCTET, OCTET, LANES), F32),
                pltpu.VMEM((2, n // OCTET, OCTET, LANES), jnp.int32),
                pltpu.VMEM((n // OCTET, OCTET, LANES), F32),
                pltpu.VMEM((n // OCTET, rows, OCTET, LANES), jnp.int32),
                pltpu.VMEM((n // OCTET, rows, OCTET, LANES), jnp.int32),
                pltpu.VMEM((2, n // OCTET, rows, OCTET, LANES), F32),
                pltpu.VMEM((n // OCTET, 4 * OCTET, LANES), F32),
                pltpu.VMEM((OCTET * 2 * n, rows // OCTET * columns), BF16),
                pltpu.VMEM((n // OCTET, OCTET, LANES), F32),
                pltpu.VMEM((depth, LANES), F32),
                pltpu.VMEM((n, depth, LANES), F32),
                pltpu.SemaphoreType.DMA((n,)),
                pltpu.SemaphoreType.DMA((n,)),
                pltpu.SemaphoreType.DMA((n,)),
                pltpu.SemaphoreType.DMA((n,)),
            ],
            compiler_params=pltpu.CompilerParams(collective_id=0, has_side_effects=True),
        )(*operands)
        return focused, correction.T

    split = ("groups", "tile")
    in_specs = (
        P(None, split, None),
        P(split, None),
        P(None, split),
        P(None, split, None),
        P(None, split, None),
        P(None, split, None),
        P(None, split, None),
    )
    out_specs = (P(None, split, None, None), P(None, split))
    return jax.shard_map(per_device, mesh=mesh, in_specs=in_specs, out_specs=out_specs, check_vma=False)
```

time: 20.3 us -> 18.9 us (0.931)
  Pallas kernels: 18.3 us -> 17 us
    pallas_call x1, Pallas kernels: 18.3 us -> 17 us  [per_device(): pl.pallas_call(functools.partial(kernel, n), out_shape=(pltpu.VMEM((2, 1,...]
where the time goes in v1:
time: 18.9 us; the launch traced here: 18.8 us
  Pallas kernels  17 us (90%)
  local copies, waits for them, and re-layouts  1.17 us (6%)
  between operations  0.64 us (3%)
    pallas_call x1, Pallas kernels, per_device(): pl.pallas_call(functools.partial(kernel, n), out_shape=(pltpu.VMEM((2, 1,...  17 us
    unnamed x2, local copies, waits for them, and re-layouts  1.17 us

profile of v1, /device:TPU:0, one launch (start us, length us, event | category | flops | bytes accessed | tf_op | source)
XLA Modules:
  0.0 18.8 jit_solution(10911790445177531729)
XLA Ops:
  0.6 17.0 %shard_map.113 = (f32[2,1,128,128]{3,2,1,0:T(8,128)S(1)}, f32[1,2]{1,0:T(1,128)S(1)}) custom-call(s32[1,16]{1,0:T(1,128)} %starts_in.1, f32[2,128,128]{2,1,0:T(8,128)} %bitcast.4, bf16[2,128,256]{2,1,0:T(8,128)(2,1)} %constant.4.clone.first_in.last_in, f32[2,128,128]{2,1,0:T(8,128)} %constant.5.clone.turn_in, ...), custom_call_target="tpu_custom_call" | custom-call | tf_op jit(solution)/shard_map/pallas_call | solution.py:356
  17.6 0.7 %copy.14 = f32[2,1,128,128]{3,2,1,0:T(8,128)} copy(f32[2,1,128,128]{3,2,1,0:T(8,128)S(1)} %get-tuple-element.6) | data formatting | bytes 262144
  18.3 0.5 %copy.15 = f32[2,1]{0,1:T(1,128)} copy(f32[2,1]{0,1:T(1,128)S(1)} %bitcast.3) | data formatting | bytes 16

commit v2 on v1

--- a/solution.py
+++ b/solution.py
@@ -67,9 +67,9 @@
 def kernel(
     n, starts_in, echo_in, first_in, turn_in, last_in, row_phase_in, column_phase_in, row_bin_in, column_bin_in,
     fraction_in,
-    focused, correction,
+    parts, weights_out, correction,
     starts, echo, first, turn, last, row_phase, column_phase, row_bin, column_bin, fraction, in_sem,
-    spec, outgoing, gathered, waves, bins_of, share, index_low, index_all, steer, windows, parts,
+    spec, outgoing, gathered, waves, share, index_all, steer, windows,
     gram_rows, message, messages,
     send_sem, recv_sem, send_sem2, recv_sem2,
 ):
@@ -148,15 +148,15 @@
         return pltpu.make_async_remote_copy(
             src_ref=outgoing.at[device],
             dst_ref=gathered.at[slot],
-            send_sem=send_sem.at[device],
-            recv_sem=recv_sem.at[slot],
+            send_sem=send_sem,
+            recv_sem=recv_sem.at[slot // OCTET],
             device_id={"tile": device},
             device_id_type=MESH,
         )
 
     for k in range(n - 1):
         window_copy(other(k), me).start()
-    gathered[me] = outgoing[me]
+    pltpu.make_async_copy(outgoing.at[me], gathered.at[me], recv_sem.at[mine]).start()
 
     def rounded(values):
         return values.astype(BF16).astype(F32)
@@ -173,28 +173,31 @@
     angles = column_phase[:, 0, :]
     waves[2] = by_octets(rounded(jnp.cos(angles)))
     waves[3] = by_octets(rounded(jnp.sin(angles)))
-    bins_of[0] = by_octets(row_bin[:, 0, :])
-    bins_of[1] = by_octets(column_bin[:, 0, :])
+    waves[4] = by_octets(row_bin[:, 0, :].astype(F32))
+    waves[5] = by_octets(column_bin[:, 0, :].astype(F32))
     octet_id = lax.broadcasted_iota(jnp.int32, (OCTET, LANES), 0)
     tiles = rows // OCTET
 
     def spread(values, u):
         return jnp.broadcast_to(values[:, u : u + 1], (OCTET, LANES))
 
+    tables = []
     for slot in range(groups):
         group = group_of(slot)
         part = jnp.zeros((OCTET, LANES), F32)
         for i in range(OCTET):
             part = jnp.where(octet_id == i, fraction[0, group * OCTET + i], part)
         share[slot] = part
-        row_cosine, row_sine = waves[0, group], waves[1, group]
-        column_cosine, column_sine = waves[2, group], waves[3, group]
-        row_index, column_index = bins_of[0, group], bins_of[1, group]
-        for u in range(rows):
-            cosine, sine = spread(row_cosine, u), spread(row_sine, u)
-            index = spread(row_index, u) + column_index
-            index_all[slot, u] = index
-            index_low[slot, u] = index & (LANES - 1)
+        tables.append([rounded(waves[q, group]) for q in range(6)])
+    column_bin_of = [table[5].astype(jnp.int32) for table in tables]
+    for u in range(rows):
+        turns = [(spread(table[0], u), spread(table[1], u)) for table in tables]
+        offsets = [spread(table[4], u) for table in tables]
+        for slot, ((cosine, sine), offset, table) in enumerate(zip(turns, offsets, tables)):
+            column_cosine, column_sine = table[2], table[3]
+            offset = offset.astype(jnp.int32)
+            index_all[0, slot, u] = (offset + column_bin_of[slot]) & (LANES - 1)
+            index_all[1, slot, u] = offset
             steer[0, slot, u] = cosine * column_cosine - sine * column_sine
             steer[1, slot, u] = cosine * column_sine + sine * column_cosine
 
@@ -210,26 +213,29 @@
             shifted = moved[q] if q % 2 else jnp.where(lane == LANES - 1, moved[q + 1], moved[q])
             profile.append(rounded((1.0 - fraction_of) * window[q] + fraction_of * shifted))
         for u in range(rows):
-            low = index_low[slot, u]
-            is_low = index_all[slot, u] < LANES
-            real = jnp.where(is_low, pick(profile[0], low), pick(profile[1], low))
-            imag = jnp.where(is_low, pick(profile[2], low), pick(profile[3], low))
+            low = index_all[0, slot, u]
+            is_low = index_all[1, slot, u] <= lane
+            real = pick(jnp.where(is_low, profile[0], profile[1]), low)
+            imag = pick(jnp.where(is_low, profile[2], profile[3]), low)
             turn_real, turn_imag = steer[0, slot, u], steer[1, slot, u]
             both = jnp.concatenate([turn_real * real - turn_imag * imag, turn_real * imag + turn_imag * real], 0)
-            top = (u % OCTET) * pair + slot * 2 * OCTET
+            top = pl.multiple_of((u % OCTET) * pair + slot * 2 * OCTET, 2 * OCTET)
             left = (u // OCTET) * LANES
-            parts[top : top + 2 * OCTET, left : left + LANES] = both.astype(BF16)
-
-    for slot in range(groups):
-        for k in range(1 if slot == 0 else 0, OCTET):
-            device = group_of(slot) * OCTET + lax.rem(me + k, OCTET)
-            window_copy(device, device).wait_recv()
+            parts[pl.ds(top, 2 * OCTET), left : left + LANES] = both.astype(BF16)
+
+    def visit(slot, carry):
+        arrived = gathered.at[pl.ds(group_of(slot) * OCTET, OCTET)]
+        pltpu.make_async_copy(arrived, arrived, recv_sem.at[group_of(slot)]).wait()
         contribute(slot)
+        return carry
+
+    lax.fori_loop(0, groups, visit, 0)
 
     total = None
-    for top in range(0, OCTET * pair, LANES):
-        values = parts[top : top + LANES, :]
+    for top in range(0, OCTET * pair, 2 * LANES):
+        values = parts[top : top + 2 * LANES, :]
         product = dot(values, values, ((1,), (1,)))
+        product = product[:LANES, :LANES] + product[LANES:, LANES:]
         total = product if total is None else total + product
     gram = total[0:pair]
     for i in range(1, LANES // pair):
@@ -261,18 +267,18 @@
         return pltpu.make_async_remote_copy(
             src_ref=message,
             dst_ref=messages.at[slot],
-            send_sem=send_sem2.at[device],
-            recv_sem=recv_sem2.at[slot],
+            send_sem=send_sem2,
+            recv_sem=recv_sem2,
             device_id={"tile": device},
             device_id_type=MESH,
         )
 
     for k in range(n - 1):
         gram_copy(other(k), me).start()
-    for k in range(n - 1):
-        window_copy(other(k), me).wait_send()
-    for k in reversed(range(n - 1)):
-        gram_copy(other(k), other(k)).wait_recv()
+    sent = outgoing.at[pl.ds(0, n - 1)]
+    pltpu.make_async_copy(sent, sent, send_sem).wait()
+    sent = messages.at[pl.ds(0, n - 1)]
+    pltpu.make_async_copy(sent, sent, recv_sem2).wait()
 
     total = jnp.sum(messages[...], axis=0)
     gram = jnp.concatenate([total] + [pltpu.roll(total, LANES - j * pair, 1) for j in range(1, folds)], 0)
@@ -324,18 +330,32 @@
     high = weights.astype(BF16)
     low = (weights - high.astype(F32)).astype(BF16)
     weights = jnp.concatenate([high, low], 0)
+    weights_out[...] = weights
+    pltpu.make_async_copy(sent, sent, send_sem2).wait()
+
+
+def image_kernel(parts, weights, correction_in, focused, correction, image, own, sem):
+    own[...] = correction_in[...]
+    copies = [pltpu.make_async_copy(own, correction, sem.at[0])]
+    copies[0].start()
     step = 2 * LANES
-    for left in range(0, tiles * LANES, step):
-        image = dot(weights, parts[:, left : left + step])
-        image = image[0 : 2 * OCTET] + image[2 * OCTET :]
-        for i in range(step // LANES):
-            t = left // LANES + i
-            span = slice(t * OCTET, (t + 1) * OCTET)
-            for h in range(2):
-                focused[h, 0, span, :] = image[h * OCTET : (h + 1) * OCTET, i * LANES : (i + 1) * LANES]
-
-    for k in range(n - 1):
-        gram_copy(other(k), me).wait_send()
+    columns = parts.shape[1]
+    chunks = 4
+    for c in range(chunks):
+        begin, end = c * columns // chunks, (c + 1) * columns // chunks
+        for left in range(begin, end, step):
+            both = dot(weights[...], parts[:, left : left + step])
+            both = both[0 : 2 * OCTET] + both[2 * OCTET :]
+            for i in range(step // LANES):
+                top = (left // LANES + i) * OCTET
+                for h in range(2):
+                    image[h, 0, top : top + OCTET, :] = both[h * OCTET : (h + 1) * OCTET, i * LANES : (i + 1) * LANES]
+        span = pl.ds(begin // LANES * OCTET, (end - begin) // LANES * OCTET)
+        copy = pltpu.make_async_copy(image.at[:, :, span], focused.at[:, :, span], sem.at[c + 1])
+        copy.start()
+        copies.append(copy)
+    for copy in copies:
+        copy.wait()
 
 
 def solution(mesh):
@@ -353,14 +373,15 @@
             row_phase, column_phase, row_bin, column_bin, bin_fraction.T,
         )
         depth = n * 2 * n // LANES
-        focused, correction = pl.pallas_call(
+        parts, weights, correction = pl.pallas_call(
             functools.partial(kernel, n),
             out_shape=(
-                pltpu.VMEM((2, 1, rows, columns), F32),
+                pltpu.VMEM((OCTET * 2 * n, rows // OCTET * columns), BF16),
+                pltpu.VMEM((4 * OCTET, OCTET * 2 * n), BF16),
                 pltpu.VMEM((1, 2), F32),
             ),
             in_specs=[pl.BlockSpec(memory_space=pltpu.HBM)] * len(operands),
-            out_specs=(vmem, vmem),
+            out_specs=(vmem, vmem, vmem),
             scratch_shapes=[pltpu.SMEM(bin_start.shape, jnp.int32)]
             + [pltpu.VMEM(operand.shape, operand.dtype) for operand in operands[1:9]]
             + [pltpu.SMEM((1, n), F32), pltpu.SemaphoreType.DMA((len(operands),))]
@@ -368,24 +389,36 @@
                 pltpu.VMEM((2, bins + OCTET, LANES), F32),
                 pltpu.VMEM((n, 4, LANES), BF16),
                 pltpu.VMEM((n, 4, LANES), BF16),
-                pltpu.VMEM((4, n // OCTET, OCTET, LANES), F32),
-                pltpu.VMEM((2, n // OCTET, OCTET, LANES), jnp.int32),
+                pltpu.VMEM((6, n // OCTET, OCTET, LANES), F32),
                 pltpu.VMEM((n // OCTET, OCTET, LANES), F32),
-                pltpu.VMEM((n // OCTET, rows, OCTET, LANES), jnp.int32),
-                pltpu.VMEM((n // OCTET, rows, OCTET, LANES), jnp.int32),
+                pltpu.VMEM((2, n // OCTET, rows, OCTET, LANES), jnp.int32),
                 pltpu.VMEM((2, n // OCTET, rows, OCTET, LANES), F32),
                 pltpu.VMEM((n // OCTET, 4 * OCTET, LANES), F32),
-                pltpu.VMEM((OCTET * 2 * n, rows // OCTET * columns), BF16),
                 pltpu.VMEM((n // OCTET, OCTET, LANES), F32),
                 pltpu.VMEM((depth, LANES), F32),
                 pltpu.VMEM((n, depth, LANES), F32),
-                pltpu.SemaphoreType.DMA((n,)),
-                pltpu.SemaphoreType.DMA((n,)),
-                pltpu.SemaphoreType.DMA((n,)),
-                pltpu.SemaphoreType.DMA((n,)),
+                pltpu.SemaphoreType.DMA(()),
+                pltpu.SemaphoreType.DMA((n // OCTET,)),
+                pltpu.SemaphoreType.DMA(()),
+                pltpu.SemaphoreType.DMA(()),
             ],
             compiler_params=pltpu.CompilerParams(collective_id=0, has_side_effects=True),
         )(*operands)
+        hbm = pl.BlockSpec(memory_space=pltpu.HBM)
+        focused, correction = pl.pallas_call(
+            image_kernel,
+            out_shape=(
+                jax.ShapeDtypeStruct((2, 1, rows, columns), F32),
+                jax.ShapeDtypeStruct((1, 2), F32),
+            ),
+            in_specs=[vmem] * 3,
+            out_specs=(hbm, hbm),
+            scratch_shapes=[
+                pltpu.VMEM((2, 1, rows, columns), F32),
+                pltpu.VMEM((1, 2), F32),
+                pltpu.SemaphoreType.DMA((5,)),
+            ],
+        )(*[pltpu.with_memory_space_constraint(x, pltpu.VMEM) for x in (parts, weights, correction)])
         return focused, correction.T
 
     split = ("groups", "tile")

time: 18.9 us -> 17.9 us (0.947)
  local copies, waits for them, and re-layouts: 1.17 us -> 0 us
    unnamed x2 -> x0, local copies, waits for them, and re-layouts: 1.17 us -> none
    pallas_call x1 -> x2, Pallas kernels: 17 us -> 17.1 us  [the longest x1 16.1 us: per_device(): pl.pallas_call(functools.partial(kernel, n), out_shape=(pltpu.VMEM((OCTET...]
where the time goes in v2:
time: 17.9 us; the launch traced here: 17.7 us
  Pallas kernels  17.1 us (96%)
  between operations  0.64 us (4%)
    pallas_call x1, Pallas kernels, per_device(): pl.pallas_call(functools.partial(kernel, n), out_shape=(pltpu.VMEM((OCTET...  16.1 us
    pallas_call x1, Pallas kernels, per_device(): pl.pallas_call(image_kernel, out_shape=(jax.ShapeDtypeStruct((2, 1, rows,...  0.95 us

profile of v2, /device:TPU:0, one launch (start us, length us, event | category | flops | bytes accessed | tf_op | source)
XLA Modules:
  0.0 17.7 jit_solution(16338660250763588439)
XLA Ops:
  0.6 16.1 %shard_map.113 = (bf16[256,2048]{1,0:T(8,128)(2,1)S(1)}, bf16[32,256]{1,0:T(8,128)(2,1)S(1)}, f32[1,2]{1,0:T(1,128)S(1)}) custom-call(s32[1,16]{1,0:T(1,128)} %starts_in.1, f32[2,128,128]{2,1,0:T(8,128)} %bitcast.3, bf16[2,128,256]{2,1,0:T(8,128)(2,1)} %constant.4.clone.first_in.last_in, f32[2,128,128]{2,1,0:T(8,128)} %constant.5.clone.turn_in, ...), custom_call_target="tpu_custom_call" | custom-call | tf_op jit(solution)/shard_map/pallas_call | solution.py:376
  16.8 0.9 %shard_map.114 = (f32[2,1,128,128]{3,2,1,0:T(8,128)}, f32[1,2]{1,0:T(1,128)}) custom-call(bf16[256,2048]{1,0:T(8,128)(2,1)S(1)} %get-tuple-element.7.parts, bf16[32,256]{1,0:T(8,128)(2,1)S(1)} %get-tuple-element.8.weights, f32[1,2]{1,0:T(1,128)S(1)} %get-tuple-element.9.correction_in), custom_call_target="tpu_custom_call" | custom-call | tf_op jit(solution)/shard_map/pallas_call | solution.py:408

commit v3 on v2

--- a/solution.py
+++ b/solution.py
@@ -50,8 +50,8 @@
 def normalize(real_part, imag_part, axis, count):
     magnitude = real_part * real_part + imag_part * imag_part
     mean = jnp.sum(magnitude, axis=axis, keepdims=True) / count
-    denominator = jnp.sqrt(magnitude + mean + 1e-06)
-    return real_part / denominator, imag_part / denominator
+    inverse = lax.rsqrt(magnitude + mean + 1e-06)
+    return real_part * inverse, imag_part * inverse
 
 
 def pick(source, index):
@@ -70,7 +70,7 @@
     parts, weights_out, correction,
     starts, echo, first, turn, last, row_phase, column_phase, row_bin, column_bin, fraction, in_sem,
     spec, outgoing, gathered, waves, share, index_all, steer, windows,
-    gram_rows, message, messages,
+    message, messages,
     send_sem, recv_sem, send_sem2, recv_sem2,
 ):
     me = lax.axis_index("tile")
@@ -167,14 +167,12 @@
     def by_octets(values):
         return values.reshape(groups, OCTET, LANES)
 
-    angles = row_phase[:, 0, :]
-    waves[0] = by_octets(rounded(jnp.cos(angles)))
-    waves[1] = by_octets(rounded(jnp.sin(angles)))
-    angles = column_phase[:, 0, :]
-    waves[2] = by_octets(rounded(jnp.cos(angles)))
-    waves[3] = by_octets(rounded(jnp.sin(angles)))
-    waves[4] = by_octets(row_bin[:, 0, :].astype(F32))
-    waves[5] = by_octets(column_bin[:, 0, :].astype(F32))
+    row_angles, column_angles = row_phase[:, 0, :], column_phase[:, 0, :]
+    for q, values in enumerate((
+        jnp.cos(row_angles), jnp.sin(row_angles), jnp.cos(column_angles), jnp.sin(column_angles),
+        row_bin[:, 0, :].astype(F32), column_bin[:, 0, :].astype(F32),
+    )):
+        waves[q] = by_octets(values)
     octet_id = lax.broadcasted_iota(jnp.int32, (OCTET, LANES), 0)
     tiles = rows // OCTET
 
@@ -182,12 +180,11 @@
         return jnp.broadcast_to(values[:, u : u + 1], (OCTET, LANES))
 
     tables = []
-    for slot in range(groups):
-        group = group_of(slot)
+    for group in range(groups):
         part = jnp.zeros((OCTET, LANES), F32)
         for i in range(OCTET):
             part = jnp.where(octet_id == i, fraction[0, group * OCTET + i], part)
-        share[slot] = part
+        share[group] = part
         tables.append([rounded(waves[q, group]) for q in range(6)])
     column_bin_of = [table[5].astype(jnp.int32) for table in tables]
     for u in range(rows):
@@ -201,65 +198,65 @@
             steer[0, slot, u] = cosine * column_cosine - sine * column_sine
             steer[1, slot, u] = cosine * column_sine + sine * column_cosine
 
-    def contribute(slot):
-        group = group_of(slot)
+    def profiles(group):
         for i in range(OCTET):
-            windows[slot, 4 * i : 4 * (i + 1), :] = gathered[group * OCTET + i].astype(F32)
-        window = [windows[slot, pl.ds(q, OCTET, stride=4), :] for q in range(4)]
+            windows[group, 4 * i : 4 * (i + 1), :] = gathered[group * OCTET + i].astype(F32)
+        window = [windows[group, pl.ds(q, OCTET, stride=4), :] for q in range(4)]
         moved = [pltpu.roll(values, LANES - 1, 1) for values in window]
-        fraction_of = share[slot]
+        fraction_of = share[group]
         profile = []
         for q in range(4):
             shifted = moved[q] if q % 2 else jnp.where(lane == LANES - 1, moved[q + 1], moved[q])
             profile.append(rounded((1.0 - fraction_of) * window[q] + fraction_of * shifted))
+        return profile
+
+    def contribute(group, profile, u):
+        low = index_all[0, group, u]
+        is_low = index_all[1, group, u] <= lane
+        real = pick(jnp.where(is_low, profile[0], profile[1]), low)
+        imag = pick(jnp.where(is_low, profile[2], profile[3]), low)
+        turn_real, turn_imag = steer[0, group, u], steer[1, group, u]
+        both = jnp.concatenate([turn_real * real - turn_imag * imag, turn_real * imag + turn_imag * real], 0)
+        top = pl.multiple_of((u % OCTET) * pair + group * 2 * OCTET, 2 * OCTET)
+        left = (u // OCTET) * LANES
+        parts[pl.ds(top, 2 * OCTET), left : left + LANES] = both.astype(BF16)
+
+    def arrive(slot):
+        group = group_of(slot)
+        arrived = gathered.at[pl.ds(group * OCTET, OCTET)]
+        pltpu.make_async_copy(arrived, arrived, recv_sem.at[group]).wait()
+        return group, profiles(group)
+
+    def visit(slot, carry):
+        group, profile = arrive(slot)
         for u in range(rows):
-            low = index_all[0, slot, u]
-            is_low = index_all[1, slot, u] <= lane
-            real = pick(jnp.where(is_low, profile[0], profile[1]), low)
-            imag = pick(jnp.where(is_low, profile[2], profile[3]), low)
-            turn_real, turn_imag = steer[0, slot, u], steer[1, slot, u]
-            both = jnp.concatenate([turn_real * real - turn_imag * imag, turn_real * imag + turn_imag * real], 0)
-            top = pl.multiple_of((u % OCTET) * pair + slot * 2 * OCTET, 2 * OCTET)
-            left = (u // OCTET) * LANES
-            parts[pl.ds(top, 2 * OCTET), left : left + LANES] = both.astype(BF16)
-
-    def visit(slot, carry):
-        arrived = gathered.at[pl.ds(group_of(slot) * OCTET, OCTET)]
-        pltpu.make_async_copy(arrived, arrived, recv_sem.at[group_of(slot)]).wait()
-        contribute(slot)
+            contribute(group, profile, u)
         return carry
 
-    lax.fori_loop(0, groups, visit, 0)
-
-    total = None
-    for top in range(0, OCTET * pair, 2 * LANES):
-        values = parts[top : top + 2 * LANES, :]
-        product = dot(values, values, ((1,), (1,)))
-        product = product[:LANES, :LANES] + product[LANES:, LANES:]
-        total = product if total is None else total + product
-    gram = total[0:pair]
-    for i in range(1, LANES // pair):
-        gram = gram + pltpu.roll(total[i * pair : (i + 1) * pair], LANES - i * pair, 1)
+    lax.fori_loop(0, groups - 1, visit, 0)
+    group, profile = arrive(groups - 1)
+    gram = jnp.zeros((pair, pair), F32)
+    for a in range(OCTET):
+        for u in range(a, rows, OCTET):
+            contribute(group, profile, u)
+        values = parts[a * pair : (a + 1) * pair, :]
+        gram = gram + dot(values, values, ((1,), (1,)))
+    gram = jnp.concatenate([gram, jnp.zeros((pair, LANES - pair), F32)], 1)
     imag_lane = (lane // OCTET) % 2 == 1
-    for slot in range(groups):
-        top = slot * 2 * OCTET
+    folds = LANES // pair
+    packed = []
+    for g in range(groups):
+        top = g * 2 * OCTET
         real, imag = gram[top : top + OCTET], gram[top + OCTET : top + 2 * OCTET]
         values = real + jnp.where(
             imag_lane, -pltpu.roll(imag, OCTET, 1), pltpu.roll(imag, LANES - OCTET, 1)
         )
         values = jnp.where(lane < pair, values, 0.0)
-        width = pair
-        while width < LANES:
-            values = values + pltpu.roll(values, width, 1)
-            width *= 2
-        gram_rows[group_of(slot)] = pltpu.roll(values, 2 * OCTET * mine, 1)
-    full = gram_rows[...].reshape(n, LANES)
-    depth = n * pair // LANES
-    folds = LANES // pair
-    block_id = lax.broadcasted_iota(jnp.int32, (depth, LANES), 1) // pair
-    packed = full[0:depth]
-    for j in range(1, folds):
-        packed = jnp.where(block_id == j, full[j * depth : (j + 1) * depth], packed)
+        if g % folds == 0:
+            packed.append(values)
+        else:
+            packed[-1] = packed[-1] + pltpu.roll(values, g % folds * pair, 1)
+    packed = jnp.concatenate(packed, 0)
     message[...] = packed
     messages[me] = packed
 
@@ -281,7 +278,12 @@
     pltpu.make_async_copy(sent, sent, recv_sem2).wait()
 
     total = jnp.sum(messages[...], axis=0)
-    gram = jnp.concatenate([total] + [pltpu.roll(total, LANES - j * pair, 1) for j in range(1, folds)], 0)
+    gram = []
+    for g in range(groups):
+        top = g // folds * OCTET
+        values = total[top : top + OCTET]
+        gram.append(values if g % folds == 0 else pltpu.roll(values, LANES - g % folds * pair, 1))
+    gram = jnp.concatenate(gram, 0)
     row_id = lax.broadcasted_iota(jnp.int32, gram.shape, 0)
     lane_id = lax.broadcasted_iota(jnp.int32, gram.shape, 1)
     column_id = lane_id // (2 * OCTET) * OCTET + lane_id % OCTET
@@ -318,7 +320,6 @@
         while width < LANES:
             values = values + pltpu.roll(values, width, 1)
             width *= 2
-        values = pltpu.roll(values, LANES - 2 * OCTET * mine, 1)
         weights.append(jnp.broadcast_to(values, (OCTET, LANES)))
     weights = jnp.concatenate(weights, 0)
     phase_id = lax.broadcasted_iota(jnp.int32, weights.shape, 0) % OCTET
@@ -372,7 +373,7 @@
             bin_start, echo, jnp.asarray(first), jnp.asarray(turn), jnp.asarray(last),
             row_phase, column_phase, row_bin, column_bin, bin_fraction.T,
         )
-        depth = n * 2 * n // LANES
+        depth = -(-n * 2 * n // (OCTET * LANES)) * OCTET
         parts, weights, correction = pl.pallas_call(
             functools.partial(kernel, n),
             out_shape=(
@@ -394,7 +395,6 @@
                 pltpu.VMEM((2, n // OCTET, rows, OCTET, LANES), jnp.int32),
                 pltpu.VMEM((2, n // OCTET, rows, OCTET, LANES), F32),
                 pltpu.VMEM((n // OCTET, 4 * OCTET, LANES), F32),
-                pltpu.VMEM((n // OCTET, OCTET, LANES), F32),
                 pltpu.VMEM((depth, LANES), F32),
                 pltpu.VMEM((n, depth, LANES), F32),
                 pltpu.SemaphoreType.DMA(()),

time: 17.9 us -> 17.4 us (0.972)
  Pallas kernels: 17.1 us -> 16.7 us
    pallas_call x1, Pallas kernels: 16.1 us -> 15.7 us  [per_device(): pl.pallas_call(functools.partial(kernel, n), out_shape=(pltpu.VMEM((OCTET...]
where the time goes in v3:
time: 17.4 us; the launch traced here: 17.3 us
  Pallas kernels  16.7 us (96%)
  between operations  0.64 us (4%)
    pallas_call x1, Pallas kernels, per_device(): pl.pallas_call(functools.partial(kernel, n), out_shape=(pltpu.VMEM((OCTET...  15.7 us
    pallas_call x1, Pallas kernels, per_device(): pl.pallas_call(image_kernel, out_shape=(jax.ShapeDtypeStruct((2, 1, rows,...  0.95 us

profile of v3, /device:TPU:0, one launch (start us, length us, event | category | flops | bytes accessed | tf_op | source)
XLA Modules:
  0.0 17.3 jit_solution(18239325070478728650)
XLA Ops:
  0.6 15.7 %shard_map.113 = (bf16[256,2048]{1,0:T(8,128)(2,1)S(1)}, bf16[32,256]{1,0:T(8,128)(2,1)S(1)}, f32[1,2]{1,0:T(1,128)S(1)}) custom-call(s32[1,16]{1,0:T(1,128)} %starts_in.1, f32[2,128,128]{2,1,0:T(8,128)} %bitcast.3, bf16[2,128,256]{2,1,0:T(8,128)(2,1)} %constant.4.clone.first_in.last_in, f32[2,128,128]{2,1,0:T(8,128)} %constant.5.clone.turn_in, ...), custom_call_target="tpu_custom_call" | custom-call | tf_op jit(solution)/shard_map/pallas_call | solution.py:377
  16.4 0.9 %shard_map.114 = (f32[2,1,128,128]{3,2,1,0:T(8,128)}, f32[1,2]{1,0:T(1,128)}) custom-call(bf16[256,2048]{1,0:T(8,128)(2,1)S(1)} %get-tuple-element.7.parts, bf16[32,256]{1,0:T(8,128)(2,1)S(1)} %get-tuple-element.8.weights, f32[1,2]{1,0:T(1,128)S(1)} %get-tuple-element.9.correction_in), custom_call_target="tpu_custom_call" | custom-call | tf_op jit(solution)/shard_map/pallas_call | solution.py:408

commit v4 on v3

--- a/solution.py
+++ b/solution.py
@@ -11,6 +11,7 @@
 
 LANES = 128
 OCTET = 8
+QUAD = 4
 MESH = pl.DeviceIdType.MESH
 F32 = jnp.float32
 BF16 = jnp.bfloat16
@@ -76,12 +77,9 @@
     me = lax.axis_index("tile")
     rows = row_phase.shape[2]
     scale = 1.0 / math.sqrt(n)
-    groups = n // OCTET
-    mine = me // OCTET
+    groups = n // QUAD
+    mine = me // QUAD
     pair = 2 * n
-
-    def group_of(slot):
-        return lax.rem(mine + slot, groups)
 
     barrier = pltpu.get_barrier_semaphore()
     for k in range(1, n):
@@ -100,6 +98,11 @@
         load.start()
 
     upper = (2 * me) // n
+
+    def group_of(slot):
+        place = upper * (groups - 1 - slot) + (1 - upper) * (slot - 1)
+        place = place + (place >= mine).astype(jnp.int32)
+        return place if isinstance(slot, int) else jnp.where(slot == 0, mine, place)
 
     def other(k):
         place = upper * k + (1 - upper) * (n - 2 - k)
@@ -149,7 +152,7 @@
             src_ref=outgoing.at[device],
             dst_ref=gathered.at[slot],
             send_sem=send_sem,
-            recv_sem=recv_sem.at[slot // OCTET],
+            recv_sem=recv_sem.at[slot // QUAD],
             device_id={"tile": device},
             device_id_type=MESH,
         )
@@ -163,33 +166,37 @@
 
     for load in loads[5:]:
         load.wait()
-
-    def by_octets(values):
-        return values.reshape(groups, OCTET, LANES)
 
     row_angles, column_angles = row_phase[:, 0, :], column_phase[:, 0, :]
     for q, values in enumerate((
         jnp.cos(row_angles), jnp.sin(row_angles), jnp.cos(column_angles), jnp.sin(column_angles),
         row_bin[:, 0, :].astype(F32), column_bin[:, 0, :].astype(F32),
     )):
-        waves[q] = by_octets(values)
+        values = values.reshape(groups, QUAD, LANES)
+        waves[q, :, 0:QUAD] = values
+        waves[q, :, QUAD:] = values
     octet_id = lax.broadcasted_iota(jnp.int32, (OCTET, LANES), 0)
     tiles = rows // OCTET
 
-    def spread(values, u):
-        return jnp.broadcast_to(values[:, u : u + 1], (OCTET, LANES))
+    pairs = [(a, t) for a in range(OCTET) for t in range(0, tiles, 2)]
+    upper_half = octet_id >= QUAD
+    second_row = jnp.where(upper_half, OCTET, 0)
+
+    def spread(values, pattern):
+        return pick(values, pattern)
 
     tables = []
     for group in range(groups):
         part = jnp.zeros((OCTET, LANES), F32)
-        for i in range(OCTET):
-            part = jnp.where(octet_id == i, fraction[0, group * OCTET + i], part)
+        for i in range(QUAD):
+            part = jnp.where(octet_id & (QUAD - 1) == i, fraction[0, group * QUAD + i], part)
         share[group] = part
         tables.append([rounded(waves[q, group]) for q in range(6)])
     column_bin_of = [table[5].astype(jnp.int32) for table in tables]
-    for u in range(rows):
-        turns = [(spread(table[0], u), spread(table[1], u)) for table in tables]
-        offsets = [spread(table[4], u) for table in tables]
+    for u, (a, t) in enumerate(pairs):
+        pattern = second_row + (t * OCTET + a)
+        turns = [(spread(table[0], pattern), spread(table[1], pattern)) for table in tables]
+        offsets = [spread(table[4], pattern) for table in tables]
         for slot, ((cosine, sine), offset, table) in enumerate(zip(turns, offsets, tables)):
             column_cosine, column_sine = table[2], table[3]
             offset = offset.astype(jnp.int32)
@@ -199,8 +206,10 @@
             steer[1, slot, u] = cosine * column_sine + sine * column_cosine
 
     def profiles(group):
-        for i in range(OCTET):
-            windows[group, 4 * i : 4 * (i + 1), :] = gathered[group * OCTET + i].astype(F32)
+        for i in range(QUAD):
+            values = gathered[group * QUAD + i].astype(F32)
+            for j in (i, i + QUAD):
+                windows[group, 4 * j : 4 * (j + 1), :] = values
         window = [windows[group, pl.ds(q, OCTET, stride=4), :] for q in range(4)]
         moved = [pltpu.roll(values, LANES - 1, 1) for values in window]
         fraction_of = share[group]
@@ -216,47 +225,61 @@
         real = pick(jnp.where(is_low, profile[0], profile[1]), low)
         imag = pick(jnp.where(is_low, profile[2], profile[3]), low)
         turn_real, turn_imag = steer[0, group, u], steer[1, group, u]
-        both = jnp.concatenate([turn_real * real - turn_imag * imag, turn_real * imag + turn_imag * real], 0)
-        top = pl.multiple_of((u % OCTET) * pair + group * 2 * OCTET, 2 * OCTET)
-        left = (u // OCTET) * LANES
-        parts[pl.ds(top, 2 * OCTET), left : left + LANES] = both.astype(BF16)
+        part_real = turn_real * real - turn_imag * imag
+        part_imag = turn_real * imag + turn_imag * real
+        a, t = pairs[u]
+        top = pl.multiple_of(a * pair + group * OCTET, OCTET)
+        both = (
+            jnp.where(upper_half, pltpu.roll(part_imag, QUAD, 0), part_real),
+            jnp.where(upper_half, part_imag, pltpu.roll(part_real, QUAD, 0)),
+        )
+        for h in range(2):
+            left = (t + h) * LANES
+            parts[pl.ds(top, OCTET), left : left + LANES] = both[h].astype(BF16)
 
     def arrive(slot):
         group = group_of(slot)
-        arrived = gathered.at[pl.ds(group * OCTET, OCTET)]
+        arrived = gathered.at[pl.ds(group * QUAD, QUAD)]
         pltpu.make_async_copy(arrived, arrived, recv_sem.at[group]).wait()
         return group, profiles(group)
 
     def visit(slot, carry):
         group, profile = arrive(slot)
-        for u in range(rows):
+        for u in range(len(pairs)):
             contribute(group, profile, u)
         return carry
 
     lax.fori_loop(0, groups - 1, visit, 0)
     group, profile = arrive(groups - 1)
-    gram = jnp.zeros((pair, pair), F32)
+    grams = [jnp.zeros((pair, pair), F32)] * 2
     for a in range(OCTET):
-        for u in range(a, rows, OCTET):
+        for u in range(a * tiles // 2, (a + 1) * tiles // 2):
             contribute(group, profile, u)
-        values = parts[a * pair : (a + 1) * pair, :]
-        gram = gram + dot(values, values, ((1,), (1,)))
-    gram = jnp.concatenate([gram, jnp.zeros((pair, LANES - pair), F32)], 1)
-    imag_lane = (lane // OCTET) % 2 == 1
+        half = tiles // 2 * LANES
+        for h in range(2):
+            values = parts[a * pair : (a + 1) * pair, h * half : (h + 1) * half]
+            grams[h] = grams[h] + dot(values, values, ((1,), (1,)))
+    gram = jnp.concatenate([grams[0] + grams[1], jnp.zeros((pair, LANES - pair), F32)], 1)
     folds = LANES // pair
-    packed = []
-    for g in range(groups):
-        top = g * 2 * OCTET
-        real, imag = gram[top : top + OCTET], gram[top + OCTET : top + 2 * OCTET]
-        values = real + jnp.where(
-            imag_lane, -pltpu.roll(imag, OCTET, 1), pltpu.roll(imag, LANES - OCTET, 1)
-        )
-        values = jnp.where(lane < pair, values, 0.0)
-        if g % folds == 0:
-            packed.append(values)
-        else:
-            packed[-1] = packed[-1] + pltpu.roll(values, g % folds * pair, 1)
-    packed = jnp.concatenate(packed, 0)
+    octets = n // OCTET
+
+    def turned(values, shift):
+        return pltpu.roll(values, shift % LANES, 1) if shift % LANES else values
+
+    packed = [jnp.zeros((OCTET, LANES), F32)] * (-(-2 * octets // folds))
+    for g in range(octets):
+        first = gram[2 * g * OCTET : (2 * g + 1) * OCTET]
+        second = gram[(2 * g + 1) * OCTET : (2 * g + 2) * OCTET]
+        real = jnp.where(upper_half, pltpu.roll(second, QUAD, 0), first)
+        imag = jnp.where(upper_half, second, pltpu.roll(first, QUAD, 0))
+        for place in (g, octets + g):
+            left = place % folds * pair
+            if place == g:
+                values = turned(real, left) + turned(imag, left - QUAD)
+            else:
+                values = turned(real, left - QUAD) - turned(imag, left)
+            packed[place // folds] = jnp.where(lane & -pair == left, values, packed[place // folds])
+    packed = jnp.concatenate([jnp.where((lane & QUAD) == 0, values, 0.0) for values in packed], 0)
     message[...] = packed
     messages[me] = packed
 
@@ -279,17 +302,16 @@
 
     total = jnp.sum(messages[...], axis=0)
     gram = []
-    for g in range(groups):
-        top = g // folds * OCTET
-        values = total[top : top + OCTET]
-        gram.append(values if g % folds == 0 else pltpu.roll(values, LANES - g % folds * pair, 1))
-    gram = jnp.concatenate(gram, 0)
+    for place in range(2 * octets):
+        top = place // folds * OCTET
+        gram.append(turned(total[top : top + OCTET], -(place % folds * pair)))
+    gram, gram_imag = jnp.concatenate(gram[:octets], 0), jnp.concatenate(gram[octets:], 0)
     row_id = lax.broadcasted_iota(jnp.int32, gram.shape, 0)
     lane_id = lax.broadcasted_iota(jnp.int32, gram.shape, 1)
-    column_id = lane_id // (2 * OCTET) * OCTET + lane_id % OCTET
-    off_diagonal = (lane_id < pair) & (lane_id // OCTET % 2 == 0) & (column_id != row_id)
+    column_id = ((lane_id >> 1) & -QUAD) + (lane_id & (QUAD - 1))
+    off_diagonal = (lane_id < pair) & ((lane_id & QUAD) == 0) & (column_id != row_id)
     gram_real = jnp.where(off_diagonal, gram * scale, 0.0)
-    gram_imag = jnp.where(off_diagonal, pltpu.roll(gram, LANES - OCTET, 1) * scale, 0.0)
+    gram_imag = jnp.where(off_diagonal, gram_imag * scale, 0.0)
 
     def along(values, axis):
         return jnp.sum(values, axis=axis, keepdims=True)
@@ -304,28 +326,24 @@
     total_real = row_real * two_real - row_imag * two_imag
     total_imag = row_real * two_imag + row_imag * two_real
     lane_row = lax.broadcasted_iota(jnp.int32, total_real.shape, 1)
-    own_lane = (me // OCTET) * 2 * OCTET + me % OCTET
+    own_lane = mine * 2 * QUAD + me % QUAD
     own = lane_row == own_lane
     correction[...] = jnp.concatenate(
         [along(jnp.where(own, total_real, 0.0), 1), along(jnp.where(own, total_imag, 0.0), 1)], 1
     )
-    row_parts = (lane_row // OCTET) % 2 == 1
     weights = []
-    for values in (
-        jnp.where(row_parts, -pltpu.roll(total_imag, OCTET, 1), total_real),
-        jnp.where(row_parts, pltpu.roll(total_real, OCTET, 1), total_imag),
-    ):
-        values = jnp.where(lane_row < pair, values * scale, 0.0)
-        width = pair
-        while width < LANES:
-            values = values + pltpu.roll(values, width, 1)
-            width *= 2
-        weights.append(jnp.broadcast_to(values, (OCTET, LANES)))
+    for straight, crossed in ((total_real, -total_imag), (total_imag, total_real)):
+        copies = []
+        for left in range(0, LANES, pair):
+            copies += [turned(straight * scale, left), turned(crossed * scale, left + QUAD)]
+        while len(copies) > 1:
+            copies = [x + y for x, y in zip(copies[::2], copies[1::2])]
+        weights.append(jnp.broadcast_to(copies[0], (OCTET, LANES)))
     weights = jnp.concatenate(weights, 0)
-    phase_id = lax.broadcasted_iota(jnp.int32, weights.shape, 0) % OCTET
+    phase_id = lax.broadcasted_iota(jnp.int32, weights.shape, 0) & (OCTET - 1)
     weight_lane = lax.broadcasted_iota(jnp.int32, weights.shape, 1)
     spans = [
-        jnp.where((weight_lane + left) // pair == phase_id, weights, 0.0) for left in range(0, OCTET * pair, LANES)
+        jnp.where((weight_lane + left) & -pair == phase_id * pair, weights, 0.0) for left in range(0, OCTET * pair, LANES)
     ]
     weights = jnp.concatenate(spans, 1)
     high = weights.astype(BF16)
@@ -373,7 +391,7 @@
             bin_start, echo, jnp.asarray(first), jnp.asarray(turn), jnp.asarray(last),
             row_phase, column_phase, row_bin, column_bin, bin_fraction.T,
         )
-        depth = -(-n * 2 * n // (OCTET * LANES)) * OCTET
+        depth = -(-4 * n * n // (OCTET * LANES)) * OCTET
         parts, weights, correction = pl.pallas_call(
             functools.partial(kernel, n),
             out_shape=(
@@ -390,15 +408,15 @@
                 pltpu.VMEM((2, bins + OCTET, LANES), F32),
                 pltpu.VMEM((n, 4, LANES), BF16),
                 pltpu.VMEM((n, 4, LANES), BF16),
-                pltpu.VMEM((6, n // OCTET, OCTET, LANES), F32),
-                pltpu.VMEM((n // OCTET, OCTET, LANES), F32),
-                pltpu.VMEM((2, n // OCTET, rows, OCTET, LANES), jnp.int32),
-                pltpu.VMEM((2, n // OCTET, rows, OCTET, LANES), F32),
-                pltpu.VMEM((n // OCTET, 4 * OCTET, LANES), F32),
+                pltpu.VMEM((6, n // QUAD, OCTET, LANES), F32),
+                pltpu.VMEM((n // QUAD, OCTET, LANES), F32),
+                pltpu.VMEM((2, n // QUAD, rows // 2, OCTET, LANES), jnp.int32),
+                pltpu.VMEM((2, n // QUAD, rows // 2, OCTET, LANES), F32),
+                pltpu.VMEM((n // QUAD, 4 * OCTET, LANES), F32),
                 pltpu.VMEM((depth, LANES), F32),
                 pltpu.VMEM((n, depth, LANES), F32),
                 pltpu.SemaphoreType.DMA(()),
-                pltpu.SemaphoreType.DMA((n // OCTET,)),
+                pltpu.SemaphoreType.DMA((n // QUAD,)),
                 pltpu.SemaphoreType.DMA(()),
                 pltpu.SemaphoreType.DMA(()),
             ],

time: 17.4 us -> 17.1 us (0.983)
  Pallas kernels: 16.7 us -> 16.3 us
    pallas_call x1, Pallas kernels: 15.7 us -> 15.4 us  [per_device(): pl.pallas_call(functools.partial(kernel, n), out_shape=(pltpu.VMEM((OCTET...]
where the time goes in v4:
time: 17.1 us; the launch traced here: 17 us
  Pallas kernels  16.3 us (95%)
  between operations  0.64 us (4%)
    pallas_call x1, Pallas kernels, per_device(): pl.pallas_call(functools.partial(kernel, n), out_shape=(pltpu.VMEM((OCTET...  15.4 us
    pallas_call x1, Pallas kernels, per_device(): pl.pallas_call(image_kernel, out_shape=(jax.ShapeDtypeStruct((2, 1, rows,...  0.95 us

profile of v4, /device:TPU:0, one launch (start us, length us, event | category | flops | bytes accessed | tf_op | source)
XLA Modules:
  0.0 17.0 jit_solution(17743186277482887253)
XLA Ops:
  0.6 15.4 %shard_map.113 = (bf16[256,2048]{1,0:T(8,128)(2,1)S(1)}, bf16[32,256]{1,0:T(8,128)(2,1)S(1)}, f32[1,2]{1,0:T(1,128)S(1)}) custom-call(s32[1,16]{1,0:T(1,128)} %starts_in.1, f32[2,128,128]{2,1,0:T(8,128)} %bitcast.3, bf16[2,128,256]{2,1,0:T(8,128)(2,1)} %constant.4.clone.first_in.last_in, f32[2,128,128]{2,1,0:T(8,128)} %constant.5.clone.turn_in, ...), custom_call_target="tpu_custom_call" | custom-call | tf_op jit(solution)/shard_map/pallas_call | solution.py:395
  16.0 0.9 %shard_map.114 = (f32[2,1,128,128]{3,2,1,0:T(8,128)}, f32[1,2]{1,0:T(1,128)}) custom-call(bf16[256,2048]{1,0:T(8,128)(2,1)S(1)} %get-tuple-element.7.parts, bf16[32,256]{1,0:T(8,128)(2,1)S(1)} %get-tuple-element.8.weights, f32[1,2]{1,0:T(1,128)S(1)} %get-tuple-element.9.correction_in), custom_call_target="tpu_custom_call" | custom-call | tf_op jit(solution)/shard_map/pallas_call | solution.py:426

commit v5 on v4

--- a/solution.py
+++ b/solution.py
@@ -48,10 +48,8 @@
     return dot(table_ref[0], high, dims) + (dot(table_ref[1], high, dims) + dot(table_ref[0], low, dims))
 
 
-def normalize(real_part, imag_part, axis, count):
-    magnitude = real_part * real_part + imag_part * imag_part
-    mean = jnp.sum(magnitude, axis=axis, keepdims=True) / count
-    inverse = lax.rsqrt(magnitude + mean + 1e-06)
+def normalize(real_part, imag_part, mean):
+    inverse = lax.rsqrt(real_part * real_part + imag_part * imag_part + mean + 1e-06)
     return real_part * inverse, imag_part * inverse
 
 
@@ -90,8 +88,9 @@
         fraction_in,
     )
     targets = (starts, echo, first, turn, last, row_phase, column_phase, row_bin, column_bin, fraction)
+    last_load = len(sources) - 1
     loads = [
-        pltpu.make_async_copy(source, target, in_sem.at[i])
+        pltpu.make_async_copy(source, target, in_sem.at[0 if i == 0 else 1 if i == last_load else 2])
         for i, (source, target) in enumerate(zip(sources, targets))
     ]
     for load in loads[1:] + loads[:1]:
@@ -109,16 +108,15 @@
         return place + (place >= me).astype(jnp.int32)
 
 
-    loads[1].wait()
-    loads[2].wait()
+    size = sum(math.prod(target.shape) * target.dtype.itemsize for target in targets[1:-1])
+    loaded = parts.at[pl.ds(0, size // (2 * parts.shape[1]))]
+    pltpu.make_async_copy(loaded, loaded, in_sem.at[2]).wait()
     real, imag = echo[0], echo[1]
     data = jnp.concatenate(
         [jnp.concatenate([real, imag], 1), jnp.concatenate([imag, -real], 1)], 0
     )
     section = split3(first, data, ((1,), (0,)))
     half = section.shape[1] // 2
-    loads[3].wait()
-    loads[4].wait()
     real, imag = section[:, :half], section[:, half:]
     turned_real = real * turn[0] + imag * turn[1]
     turned_imag = imag * turn[0] - real * turn[1]
@@ -164,8 +162,7 @@
     def rounded(values):
         return values.astype(BF16).astype(F32)
 
-    for load in loads[5:]:
-        load.wait()
+    loads[-1].wait()
 
     row_angles, column_angles = row_phase[:, 0, :], column_phase[:, 0, :]
     for q, values in enumerate((
@@ -301,36 +298,36 @@
     pltpu.make_async_copy(sent, sent, recv_sem2).wait()
 
     total = jnp.sum(messages[...], axis=0)
-    gram = []
-    for place in range(2 * octets):
-        top = place // folds * OCTET
-        gram.append(turned(total[top : top + OCTET], -(place % folds * pair)))
-    gram, gram_imag = jnp.concatenate(gram[:octets], 0), jnp.concatenate(gram[octets:], 0)
-    row_id = lax.broadcasted_iota(jnp.int32, gram.shape, 0)
-    lane_id = lax.broadcasted_iota(jnp.int32, gram.shape, 1)
-    column_id = ((lane_id >> 1) & -QUAD) + (lane_id & (QUAD - 1))
-    off_diagonal = (lane_id < pair) & ((lane_id & QUAD) == 0) & (column_id != row_id)
-    gram_real = jnp.where(off_diagonal, gram * scale, 0.0)
-    gram_imag = jnp.where(off_diagonal, gram_imag * scale, 0.0)
-
     def along(values, axis):
         return jnp.sum(values, axis=axis, keepdims=True)
 
-    one_real, one_imag = normalize(along(gram_real, 1), along(gram_imag, 1), 0, n)
-    row_real, row_imag = normalize(along(gram_real, 0), -along(gram_imag, 0), 1, n)
+    inner = lane & (pair - 1)
+    column_id = ((inner >> 1) & -QUAD) + (inner & (QUAD - 1))
+    gram, near = [], []
+    for place in range(2 * octets):
+        top, left = place // folds * OCTET, place % folds * pair
+        kept = column_id != octet_id + place % octets * OCTET
+        values = jnp.where(kept, total[top : top + OCTET] * scale, 0.0)
+        sums = along(jnp.where(lane & -pair == left, values, 0.0), 1)
+        near.append(jnp.broadcast_to(sums, (OCTET, LANES)))
+        gram.append(jnp.where(lane < pair, turned(values, -left), 0.0))
+    gram_real, gram_imag = jnp.concatenate(gram[:octets], 0), jnp.concatenate(gram[octets:], 0)
+    near_real, near_imag = jnp.concatenate(near[:octets], 0), jnp.concatenate(near[octets:], 0)
+    mean = along(near_real * near_real + near_imag * near_imag, 0) / n
+    one_real, one_imag = normalize(near_real, near_imag, mean)
+    row_real, row_imag = normalize(along(gram_real, 0), -along(gram_imag, 0), mean)
     rest_real = along(gram_real * one_real + gram_imag * one_imag, 0)
     rest_imag = along(gram_real * one_imag - gram_imag * one_real, 0)
     again_real = row_real * rest_real + row_imag * rest_imag
     again_imag = row_real * rest_imag - row_imag * rest_real
-    two_real, two_imag = normalize(again_real, again_imag, 1, n)
+    mean = jnp.broadcast_to(along(again_real * again_real + again_imag * again_imag, 1), (1, LANES)) / n
+    two_real, two_imag = normalize(again_real, again_imag, mean)
     total_real = row_real * two_real - row_imag * two_imag
     total_imag = row_real * two_imag + row_imag * two_real
     lane_row = lax.broadcasted_iota(jnp.int32, total_real.shape, 1)
     own_lane = mine * 2 * QUAD + me % QUAD
     own = lane_row == own_lane
-    correction[...] = jnp.concatenate(
-        [along(jnp.where(own, total_real, 0.0), 1), along(jnp.where(own, total_imag, 0.0), 1)], 1
-    )
+    correction[...] = jnp.concatenate([jnp.where(own, total_real, 0.0), jnp.where(own, total_imag, 0.0)], 0)
     weights = []
     for straight, crossed in ((total_real, -total_imag), (total_imag, total_real)):
         copies = []
@@ -354,9 +351,7 @@
 
 
 def image_kernel(parts, weights, correction_in, focused, correction, image, own, sem):
-    own[...] = correction_in[...]
-    copies = [pltpu.make_async_copy(own, correction, sem.at[0])]
-    copies[0].start()
+    copies = []
     step = 2 * LANES
     columns = parts.shape[1]
     chunks = 4
@@ -373,6 +368,11 @@
         copy = pltpu.make_async_copy(image.at[:, :, span], focused.at[:, :, span], sem.at[c + 1])
         copy.start()
         copies.append(copy)
+        if c == 0:
+            sums = jnp.sum(correction_in[...], axis=1, keepdims=True)
+            own[...] = jnp.concatenate([sums[0:1], sums[1:2]], 1)
+            copies.append(pltpu.make_async_copy(own, correction, sem.at[0]))
+            copies[-1].start()
     for copy in copies:
         copy.wait()
 
@@ -397,13 +397,13 @@
             out_shape=(
                 pltpu.VMEM((OCTET * 2 * n, rows // OCTET * columns), BF16),
                 pltpu.VMEM((4 * OCTET, OCTET * 2 * n), BF16),
-                pltpu.VMEM((1, 2), F32),
+                pltpu.VMEM((2, LANES), F32),
             ),
             in_specs=[pl.BlockSpec(memory_space=pltpu.HBM)] * len(operands),
             out_specs=(vmem, vmem, vmem),
             scratch_shapes=[pltpu.SMEM(bin_start.shape, jnp.int32)]
             + [pltpu.VMEM(operand.shape, operand.dtype) for operand in operands[1:9]]
-            + [pltpu.SMEM((1, n), F32), pltpu.SemaphoreType.DMA((len(operands),))]
+            + [pltpu.SMEM((1, n), F32), pltpu.SemaphoreType.DMA((3,))]
             + [
                 pltpu.VMEM((2, bins + OCTET, LANES), F32),
                 pltpu.VMEM((n, 4, LANES), BF16),

time: 17.1 us -> 17 us (level)
  no operation moved by 1% of the time
where the time goes in v5:
time: 17 us; the launch traced here: 16.9 us
  Pallas kernels  16.2 us (95%)
  between operations  0.64 us (4%)
    pallas_call x1, Pallas kernels, per_device(): pl.pallas_call(functools.partial(kernel, n), out_shape=(pltpu.VMEM((OCTET...  15.3 us
    pallas_call x1, Pallas kernels, per_device(): pl.pallas_call(image_kernel, out_shape=(jax.ShapeDtypeStruct((2, 1, rows,...  0.95 us

profile of v5, /device:TPU:0, one launch (start us, length us, event | category | flops | bytes accessed | tf_op | source)
XLA Modules:
  0.0 16.9 jit_solution(14782627432029474955)
XLA Ops:
  0.6 15.3 %shard_map.113 = (bf16[256,2048]{1,0:T(8,128)(2,1)S(1)}, bf16[32,256]{1,0:T(8,128)(2,1)S(1)}, f32[2,128]{1,0:T(2,128)S(1)}) custom-call(s32[1,16]{1,0:T(1,128)} %starts_in.1, f32[2,128,128]{2,1,0:T(8,128)} %bitcast.3, bf16[2,128,256]{2,1,0:T(8,128)(2,1)} %constant.4.clone.first_in.last_in, f32[2,128,128]{2,1,0:T(8,128)} %constant.5.clone.turn_in, ...), custom_call_target="tpu_custom_call" | custom-call | tf_op jit(solution)/shard_map/pallas_call | solution.py:395
  15.9 1.0 %shard_map.114 = (f32[2,1,128,128]{3,2,1,0:T(8,128)}, f32[1,2]{1,0:T(1,128)}) custom-call(bf16[256,2048]{1,0:T(8,128)(2,1)S(1)} %get-tuple-element.7.parts, bf16[32,256]{1,0:T(8,128)(2,1)S(1)} %get-tuple-element.8.weights, f32[2,128]{1,0:T(2,128)S(1)} %get-tuple-element.9.correction_in), custom_call_target="tpu_custom_call" | custom-call | tf_op jit(solution)/shard_map/pallas_call | solution.py:426

commit v6 on v5

--- a/solution.py
+++ b/solution.py
@@ -80,8 +80,10 @@
     pair = 2 * n
 
     barrier = pltpu.get_barrier_semaphore()
-    for k in range(1, n):
-        pl.semaphore_signal(barrier, inc=1, device_id={"tile": lax.rem(me + k, n)}, device_id_type=MESH)
+    for k in range(n - 1):
+        place = (2 * me) // n * k + (1 - (2 * me) // n) * (n - 2 - k)
+        far = place + (place >= me).astype(jnp.int32)
+        pl.semaphore_signal(barrier, inc=1, device_id={"tile": far}, device_id_type=MESH)
 
     sources = (
         starts_in, echo_in, first_in, turn_in, last_in, row_phase_in, column_phase_in, row_bin_in, column_bin_in,
@@ -297,7 +299,10 @@
     sent = messages.at[pl.ds(0, n - 1)]
     pltpu.make_async_copy(sent, sent, recv_sem2).wait()
 
-    total = jnp.sum(messages[...], axis=0)
+    terms = [messages[i] for i in range(n)]
+    while len(terms) > 1:
+        terms = [x + y for x, y in zip(terms[::2], terms[1::2])]
+    total = terms[0]
     def along(values, axis):
         return jnp.sum(values, axis=axis, keepdims=True)
 

time: 17 us -> 17 us (level)
  no operation moved by 1% of the time
where the time goes in v6:
time: 17 us; the launch traced here: 16.8 us
  Pallas kernels  16.2 us (95%)
  between operations  0.64 us (4%)
    pallas_call x1, Pallas kernels, per_device(): pl.pallas_call(functools.partial(kernel, n), out_shape=(pltpu.VMEM((OCTET...  15.3 us
    pallas_call x1, Pallas kernels, per_device(): pl.pallas_call(image_kernel, out_shape=(jax.ShapeDtypeStruct((2, 1, rows,...  0.95 us

profile of v6, /device:TPU:0, one launch (start us, length us, event | category | flops | bytes accessed | tf_op | source)
XLA Modules:
  0.0 16.8 jit_solution(11733902678725925138)
XLA Ops:
  0.6 15.3 %shard_map.113 = (bf16[256,2048]{1,0:T(8,128)(2,1)S(1)}, bf16[32,256]{1,0:T(8,128)(2,1)S(1)}, f32[2,128]{1,0:T(2,128)S(1)}) custom-call(s32[1,16]{1,0:T(1,128)} %starts_in.1, f32[2,128,128]{2,1,0:T(8,128)} %bitcast.3, bf16[2,128,256]{2,1,0:T(8,128)(2,1)} %constant.4.clone.first_in.last_in, f32[2,128,128]{2,1,0:T(8,128)} %constant.5.clone.turn_in, ...), custom_call_target="tpu_custom_call" | custom-call | tf_op jit(solution)/shard_map/pallas_call | solution.py:400
  15.9 1.0 %shard_map.114 = (f32[2,1,128,128]{3,2,1,0:T(8,128)}, f32[1,2]{1,0:T(1,128)}) custom-call(bf16[256,2048]{1,0:T(8,128)(2,1)S(1)} %get-tuple-element.7.parts, bf16[32,256]{1,0:T(8,128)(2,1)S(1)} %get-tuple-element.8.weights, f32[2,128]{1,0:T(2,128)S(1)} %get-tuple-element.9.correction_in), custom_call_target="tpu_custom_call" | custom-call | tf_op jit(solution)/shard_map/pallas_call | solution.py:431
